TPU v7x, 32 devices: a whole 2x2x4 slice. The times are simulated.
32 devices in a mesh: pix: 32 (over z, y, x, core).
Axes of the slice: x: 2, y: 2, z: 4, core: 2. Of those that a mesh axis runs over, the one named last changes fastest.
Arguments:
- green: float32 [2048, 6144], P('pix'), may hold values from -200 to 200, as said below
- sketch: float32 [6144, 128], P('pix'), may hold values from -0.078125 to 0.078125
Outputs:
- basis: float32 [2048, 128], P('pix')
- projection: float32 [6144, 128], P('pix')
- spectrum_gram: float32 [128, 128], replicated
Inputs may be any that keep to these rules, and one draw needn't show every extreme that they name: `green`: finite real entries; each patch's column has its own scale.
All inputs are finite; a program needn't handle non-finite values.
Results may differ from a plain program's by a relative error of at most 0.000086.
Values sent between devices are 32-bit elements; how exact they have to be, the bound alone decides.
A program may use at most 64 MiB of HBM per device.

v0:
```python
import jax
import jax.numpy as jnp
from jax import lax
from jax.sharding import PartitionSpec as P

PATCHES = 6144


def body(green, sketch):
    highest = lax.Precision.HIGHEST
    rows_here = green.shape[0]
    devices_pix = lax.axis_size("pix")
    total_pixels = rows_here * devices_pix
    columns = green
    sketched = jnp.dot(
        columns,
        lax.all_gather(sketch, "pix", axis=0, tiled=True),
        precision=highest,
        preferred_element_type=jnp.float32,
    )
    local_gram = jnp.dot(
        sketched.T, sketched, precision=highest, preferred_element_type=jnp.float32
    )
    columns = green
    raw_proj = lax.psum_scatter(
        lax.dot_general(
            columns,
            sketched,
            (((0,), (0,)), ((), ())),
            precision=highest,
            preferred_element_type=jnp.float32,
        ),
        "pix",
        scatter_dimension=0,
        tiled=True,
    )
    gram = lax.psum(local_gram, "pix")
    lower = jnp.linalg.cholesky(gram)
    orthonormal = jax.scipy.linalg.solve_triangular(lower, sketched.T, lower=True).T
    projection = jax.scipy.linalg.solve_triangular(lower, raw_proj.T, lower=True).T
    basis = jnp.sqrt(jnp.float32(total_pixels)) * orthonormal
    local_spec = jnp.dot(
        projection.T, projection, precision=highest, preferred_element_type=jnp.float32
    )
    spectrum_gram = lax.psum(local_spec, "pix") / jnp.float32(PATCHES)
    return (basis, projection, spectrum_gram)


def solution(mesh):
    in_specs = (P("pix", None), P("pix", None))
    out_specs = (P("pix", None), P("pix", None), P())
    return jax.shard_map(body, mesh=mesh, in_specs=in_specs, out_specs=out_specs, check_vma=False)
```

profile of v0, /device:TPU:0, one launch (start us, length us, event | category | flops | bytes accessed | tf_op | source)
XLA Modules:
  0.0 438.3 jit_solution(5103394524616839399)
XLA Ops:
  7.2 0.0 all-gather.2.cloned.1.call-start
  7.2 0.7 all-gather.2.cloned.1.call-update
  7.9 0.0 all-reduce.3.cloned.1.call-start
  8.0 64.7 %all-gather.2.cloned.1.call-done = f32[6144,128]{1,0:T(8,128)} async-done(((f32[192,128]{1,0:T(8,128)}), f32[6144,128]{1,0:T(8,128)}) %all-gather.2.cloned.1.call-update) | async-done | bytes 3145744 | tf_op jit(solution)/shard_map/all_gather | solution.py:17
  72.7 3.9 fusion.5
  76.6 0.9 fusion.6
  77.5 0.0 all-reduce.3.cloned.1.call-update
  77.5 0.0 reduce-scatter.4.cloned.1.call-start
  77.6 4.4 convolution_bitcast_fusion
  81.9 3.6 copy.10
  85.5 0.2 all-reduce.5.cloned.1.call-start
  85.8 111.2 %all-reduce.3.cloned.1.call-done = f32[128,128]{0,1:T(8,128)} async-done(((f32[128,128]{0,1:T(8,128)}), f32[128,128]{0,1:T(8,128)}) %all-reduce.3.cloned.1.call-update) | async-done | bytes 65552 | tf_op jit(solution)/shard_map/psum | solution.py:37
  197.0 0.9 copy.8
  197.9 0.9 fusion.4
  198.8 11.7 %cholesky.16 = f32[128,128]{1,0:T(8,128)S(1)} custom-call(f32[128,128]{1,0:T(8,128)S(1)} %fusion.4), custom_call_target="Cholesky" | custom-call | tf_op jit(solution)/shard_map/jit(cholesky)/cholesky | solution.py:38
  210.5 0.6 compare_reduce_fusion
  211.1 0.7 fusion
  211.8 9.8 %custom-call.10 = f32[1,128,128]{1,2,0:T(8,128)S(1)} custom-call(f32[1,128,128]{2,1,0:T(8,128)S(1)} %fusion), custom_call_target="InvertDiagBlocksLowerTriangular" | custom-call | tf_op jit(solution)/shard_map/jit(_solve_triangular)/triangular_solve | solution.py:39
  221.6 84.3 %reduce-scatter.4.cloned.1.call-done = f32[192,128]{1,0:T(8,128)} async-done(((f32[6144,128]{1,0:T(8,128)}), f32[192,128]{1,0:T(8,128)}) %reduce-scatter.4.cloned.1.call-update) | async-done | bytes 98320
  305.9 1.1 fusion.1
  307.1 1.1 fusion.7
  308.2 0.8 convolution_multiply_fusion
  309.0 121.3 %all-reduce.5.cloned.1.call-done = f32[128,128]{1,0:T(8,128)} async-done(((f32[128,128]{1,0:T(8,128)}), f32[128,128]{1,0:T(8,128)}) %all-reduce.5.cloned.1.call-update) | async-done | bytes 65552 | tf_op jit(solution)/shard_map/psum | solution.py:45
  430.3 1.5 broadcast_multiply_fusion
  (7 shorter events, 0.1 us)
Async XLA Ops:
  7.2 65.5 %copy-start = (f32[64,6144]{1,0:T(8,128)S(1)}, f32[64,6144]{1,0:T(8,128)}, u32[]{:S(2)}) copy-start(f32[64,6144]{1,0:T(8,128)} %param.2) | copy-start | bytes 4718596
  7.2 65.5 %all-gather.2.cloned.1.call-start = ((), (), s32[]{:S(2)}) async-start(), calls=%async_computation.1 | async-start | bytes 3244032 | tf_op jit(solution)/shard_map/all_gather | solution.py:17
  7.9 189.0 %all-reduce.3.cloned.1.call-start = ((), (), s32[]{:S(2)}) async-start(), calls=%async_computation.2 | async-start | bytes 131072 | tf_op jit(solution)/shard_map/psum | solution.py:37
  77.5 228.4 %reduce-scatter.4.cloned.1.call-start = ((), (), s32[]{:S(2)}) async-start(), calls=%async_computation.4 | async-start | bytes 3244032
  85.5 344.8 %all-reduce.5.cloned.1.call-start = ((), (), s32[]{:S(2)}) async-start(), calls=%async_computation.3 | async-start | bytes 131072 | tf_op jit(solution)/shard_map/psum | solution.py:45
  307.1 124.7 %copy-start.1 = (f32[128,192]{0,1:T(8,128)}, f32[128,192]{0,1:T(8,128)S(1)}, u32[]{:S(2)}) copy-start(f32[128,192]{0,1:T(8,128)S(1)} %fusion.1) | copy-start | bytes 294916
Sparse Core Ops, SparseCore 0:
  10.9 61.7 all-gather.1
  78.8 118.0 all-reduce.2
  202.4 103.4 reduce-scatter.3
  311.9 118.3 all-reduce.4
where the time goes:
time: 440 us; the launch traced here: 438 us
  waiting for transfers between devices  382 us (87%)
  other arithmetic  25.2 us (6%)
  between operations  13.8 us (3%)
  matrix products  12.2 us (3%)
  local copies, waits for them, and re-layouts  4.5 us (1%)
    psum x1, waiting for transfers between devices, body(): spectrum_gram = lax.psum(local_spec, 'pix') / jnp.float32(PATCHES)  121 us
    psum x1, waiting for transfers between devices, body(): gram = lax.psum(local_gram, 'pix')  111 us
    unnamed x5, waiting for transfers between devices  85 us
    all_gather x1, waiting for transfers between devices, body(): lax.all_gather(sketch, 'pix', axis=0, tiled=True)  64.7 us
    another operation x3, other arithmetic, body(): lower = jnp.linalg.cholesky(gram)  12.4 us
    another operation x2, other arithmetic, body(): jax.scipy.linalg.solve_triangular(lower, sketched.T, lower=True)  10.5 us
  transfers between devices with their start and end apart: 4, of which 4 were waited for; matrix products, arithmetic and copies ran while one was open for 8% of the time, Pallas kernels for 0%

commit v1 on v0

v1 whole, which is shorter than its diff:
```python
import functools

import jax
import jax.numpy as jnp
from jax import lax
from jax.experimental import pallas as pl
from jax.experimental.pallas import tpu as pltpu
from jax.sharding import PartitionSpec as P

MESH = pl.DeviceIdType.MESH
F32 = jnp.float32
BF16 = jnp.bfloat16
CHUNKS = 4


def grid_of(devices):
    cores = 2 if devices % 2 == 0 else 1
    chips = devices // cores
    side = 1
    for k in range(1, chips + 1):
        if chips % (k * k) == 0 and k * k * k <= chips:
            side = k
    return cores, side, side, chips // (side * side)


def split(v):
    hi = v.astype(BF16)
    return hi, (v - hi.astype(F32)).astype(BF16)


def dot(a, b, dims=((1,), (0,))):
    return lax.dot_general(a, b, (dims, ((), ())), preferred_element_type=F32)


def exact(a, b, dims=((1,), (0,))):
    return lax.dot_general(
        a, b, (dims, ((), ())), precision=lax.Precision.HIGHEST, preferred_element_type=F32
    )


def kernel(grid, total_pixels, patches, green, sketch, basis, projection, spectrum, scratch):
    C, X, Y, Z = grid
    assert C == 2
    r = scratch
    me = lax.axis_index("pix")
    c = lax.rem(me, C)
    x = lax.rem(me // C, X)
    y = lax.rem(me // (C * X), Y)
    z = me // (C * X * Y)
    rows = sketch.shape[0]
    rank = sketch.shape[1]
    pixels = green.shape[0]
    half_a = (rows // 2 + 7) // 8 * 8
    part_a, part_b = pl.ds(0, half_a), pl.ds(half_a, rows - half_a)
    slab = X * Y * C * rows

    def dev(zz, yy, xx, cc):
        return (((zz * Y + yy) * X + xx) * C + cc,)

    def at(v, d, n):
        return lax.rem(v + d + n, n)

    partner = dev(z, y, x, 1 - c)
    counter = [0]
    sends = []

    def copy(src, dst, recv, to):
        d = pltpu.make_async_remote_copy(
            src_ref=src, dst_ref=dst, send_sem=r["send"].at[counter[0]], recv_sem=recv,
            device_id=to, device_id_type=MESH,
        )
        counter[0] += 1
        sends.append(d)
        d.start()

    def arrive(dst, recv):
        pltpu.make_async_remote_copy(
            src_ref=dst, dst_ref=dst, send_sem=r["send"].at[0], recv_sem=recv,
            device_id=partner, device_id_type=MESH,
        ).wait_recv()

    barrier = pltpu.get_barrier_semaphore()
    plane = [(dy, dx) for dy in range(Y) for dx in range(X) if (dy, dx) != (0, 0)]
    peers = [partner]
    peers += [dev(z, at(y, dy, Y), at(x, dx, X), c) for dy, dx in plane]
    peers += [dev(at(z, d, Z), y, x, c) for d in range(1, Z)]
    for peer in peers:
        pl.semaphore_signal(barrier, inc=1, device_id=peer, device_id_type=MESH)
    pl.semaphore_wait(barrier, len(peers))

    near_first = sorted(range(1, Z), key=lambda d: min(d, Z - d))

    gat = r["gat"]
    slabs = [0] + near_first

    def ag1(s):
        zc = at(z, s, Z)
        if s == 0:
            mine_a, mine_b = sketch.at[part_a], sketch.at[part_b]
        else:
            arrive(gat.at[zc, y, x, c], r["agz"].at[s])
            mine_a, mine_b = gat.at[zc, y, x, c, part_a], gat.at[zc, y, x, c, part_b]
        for dx in range(1, X):
            copy(mine_a, gat.at[zc, y, x, c, part_a], r["agxa"].at[s, dx],
                 dev(z, y, at(x, dx, X), c))
        for dy in range(1, Y):
            copy(mine_b, gat.at[zc, y, x, c, part_b], r["agyb"].at[s, dy],
                 dev(z, at(y, dy, Y), x, c))
        if s == 0:
            for d in near_first:
                copy(sketch, gat.at[z, y, x, c], r["agz"].at[d], dev(at(z, -d, Z), y, x, c))
            gat[z, y, x, c] = sketch[...]

    def ag2(s):
        zc = at(z, s, Z)
        for dx in range(1, X):
            arrive(gat.at[zc, y, at(x, -dx, X), c, part_a], r["agxa"].at[s, dx])
        for dy in range(1, Y):
            ref = gat.at[zc, y, :, c, part_a]
            copy(ref, ref, r["agya"].at[s, dy], dev(z, at(y, dy, Y), x, c))
        for dy in range(1, Y):
            arrive(gat.at[zc, at(y, -dy, Y), x, c, part_b], r["agyb"].at[s, dy])
        for dx in range(1, X):
            ref = gat.at[zc, :, x, c, part_b]
            copy(ref, ref, r["agxb"].at[s, dx], dev(z, y, at(x, dx, X), c))

    def ag3(s):
        zc = at(z, s, Z)
        for dy in range(1, Y):
            arrive(gat.at[zc, at(y, -dy, Y), :, c, part_a], r["agya"].at[s, dy])
        for dx in range(1, X):
            arrive(gat.at[zc, :, at(x, -dx, X), c, part_b], r["agxb"].at[s, dx])
        ref = gat.at[zc, :, :, c]
        copy(ref, ref, r["agd"].at[s], partner)

    def ag4(s):
        zc = at(z, s, Z)
        arrive(gat.at[zc, :, :, 1 - c], r["agd"].at[s])
        block = gat[zc].reshape(slab, rank)
        g = green[:, pl.ds(pl.multiple_of(zc * slab, 128), slab)]
        g_hi, g_lo = split(g)
        b_hi, b_lo = split(block)
        both = dot(jnp.concatenate([g_hi, g_lo], axis=0), b_hi)
        out = both[:pixels] + both[pixels:] + dot(g_hi, b_lo)
        if s == 0:
            r["sketched"][...] = out
        else:
            r["sketched"][...] += out

    def pipeline(stages, items, extra=()):
        extra = list(extra)
        for t in range(len(items) + len(stages) - 1):
            for k, stage in enumerate(stages):
                if 0 <= t - k < len(items):
                    stage(items[t - k])
            if t > 0 and extra:
                extra.pop(0)()
        return extra

    pipeline([ag1, ag2, ag3, ag4], slabs)
    sketched = r["sketched"][...]
    s_hi, s_lo = split(sketched)
    packed = jnp.concatenate([s_hi, s_lo, s_hi, s_lo], axis=0)

    def all_sum(k, value, out):
        inc, mid, top = r["ar_in"].at[k], r["ar_mid"].at[k], r["ar_top"].at[k]
        h = rank // C
        keep = pl.ds(pl.multiple_of(c * h, h), h)
        give = pl.ds(pl.multiple_of((1 - c) * h, h), h)
        here = y * X + x

        def step0():
            r["ar_src"][k] = value()
            copy(r["ar_src"].at[k, give], inc, r["ar0"].at[k], partner)

        def step1():
            arrive(inc, r["ar0"].at[k])
            mid[here] = r["ar_src"][k, keep] + inc[...]
            for i, (dy, dx) in enumerate(plane):
                copy(mid.at[here], mid.at[here], r["ar1"].at[k, i],
                     dev(z, at(y, dy, Y), at(x, dx, X), c))

        def step2():
            for i, (dy, dx) in enumerate(plane):
                arrive(mid.at[at(y, -dy, Y) * X + at(x, -dx, X)], r["ar1"].at[k, i])
            top[z] = jnp.sum(mid[...], axis=0)
            for d in near_first:
                copy(top.at[z], top.at[z], r["ar2"].at[k, d], dev(at(z, d, Z), y, x, c))

        def step3():
            for d in near_first:
                arrive(top.at[at(z, -d, Z)], r["ar2"].at[k, d])
            out[keep, :] = jnp.sum(top[...], axis=0)
            copy(out.at[keep], out.at[keep], r["ar3"].at[k], partner)

        def step4():
            arrive(out.at[give], r["ar3"].at[k])

        return [step0, step1, step2, step3, step4]

    aug = r["aug"]
    lane = lax.broadcasted_iota(jnp.int32, (rank, rank), 1)
    row_of = lax.broadcasted_iota(jnp.int32, (rank, rank), 0)

    def eliminate(j, _):
        row = aug[pl.ds(j, 1), :]
        left = aug[:, :rank]
        col = jnp.sum(jnp.where(lane == j, left, 0.0), axis=1, keepdims=True)
        pivot = jnp.sum(jnp.where(lane[:1] == j, row[:, :rank], 0.0), axis=1, keepdims=True)
        f = jnp.where(row_of[:, :1] > j, col * (1.0 / pivot), 0.0)
        aug[...] = aug[...] - f * row
        return 0

    def chol(i):
        def run():
            if i == 0:
                aug[:, :rank] = r["gram"][...]
                aug[:, rank:] = jnp.where(lane == row_of, 1.0, 0.0)
            lax.fori_loop(rank // CHUNKS * i, rank // CHUNKS * (i + 1), eliminate, 0)

        return run

    part, q = r["part"], r["q"]

    def rs1(s):
        zo = at(z, s, Z)
        g_hi, g_lo = split(green[:, pl.ds(pl.multiple_of(zo * slab, 128), slab)])
        tall = jnp.concatenate([g_hi, g_hi, g_lo, g_lo], axis=0)
        part[s] = dot(tall, packed, ((0,), (0,))).reshape(Y, X, C, rows, rank)
        copy(part.at[s, :, :, 1 - c], r["rd"].at[s], r["rsd"].at[s], partner)

    def rs2(s):
        arrive(r["rd"].at[s], r["rsd"].at[s])
        q[s] = part[s, :, :, c] + r["rd"][s]
        for dy in range(1, Y):
            copy(q.at[s, at(y, dy, Y), :, part_a], r["rya"].at[s, dy], r["rsya"].at[s, dy],
                 dev(z, at(y, dy, Y), x, c))
        for dx in range(1, X):
            copy(q.at[s, :, at(x, dx, X), part_b], r["rxb"].at[s, dx], r["rsxb"].at[s, dx],
                 dev(z, y, at(x, dx, X), c))

    def rs3(s):
        total = q[s, y, :, part_a]
        for dy in range(1, Y):
            arrive(r["rya"].at[s, dy], r["rsya"].at[s, dy])
            total = total + r["rya"][s, dy]
        r["qa"][s] = total
        for dx in range(1, X):
            copy(r["qa"].at[s, at(x, dx, X)], r["rxa"].at[s, dx], r["rsxa"].at[s, dx],
                 dev(z, y, at(x, dx, X), c))
        total = q[s, :, x, part_b]
        for dx in range(1, X):
            arrive(r["rxb"].at[s, dx], r["rsxb"].at[s, dx])
            total = total + r["rxb"][s, dx]
        r["qb"][s] = total
        for dy in range(1, Y):
            copy(r["qb"].at[s, at(y, dy, Y)], r["ryb"].at[s, dy], r["rsyb"].at[s, dy],
                 dev(z, at(y, dy, Y), x, c))

    def rs4(s):
        total = r["qa"][s, x]
        for dx in range(1, X):
            arrive(r["rxa"].at[s, dx], r["rsxa"].at[s, dx])
            total = total + r["rxa"][s, dx]
        r["fin"][s, part_a] = total
        total = r["qb"][s, y]
        for dy in range(1, Y):
            arrive(r["ryb"].at[s, dy], r["rsyb"].at[s, dy])
            total = total + r["ryb"][s, dy]
        r["fin"][s, part_b] = total
        if s:
            copy(r["fin"].at[s], r["rz"].at[s], r["rsz"].at[s], dev(at(z, s, Z), y, x, c))

    gram_sum = all_sum(0, lambda: exact(sketched, sketched, ((0,), (0,))), r["gram"])
    gram_sum[0]()
    todo = gram_sum[1:] + [chol(i) for i in range(CHUNKS)]
    todo = pipeline([rs1, rs2, rs3, rs4], near_first[::-1] + [0], todo)

    raw = r["fin"][0]
    for s in range(1, Z):
        arrive(r["rz"].at[s], r["rsz"].at[s])
        raw = raw + r["rz"][s]
    spec_sum = all_sum(1, lambda: exact(raw, raw, ((0,), (0,))), r["spec"])
    for k, step in enumerate(spec_sum):
        step()
        if todo:
            todo.pop(0)()
    for job in todo:
        job()

    diag = jnp.sum(jnp.where(lane == row_of, aug[:, :rank], 0.0), axis=1, keepdims=True)
    inverse = aug[:, rank:] * lax.rsqrt(diag)
    basis[...] = jnp.sqrt(F32(total_pixels)) * exact(sketched, inverse, ((1,), (1,)))
    projection[...] = exact(raw, inverse, ((1,), (1,)))
    spectrum[...] = exact(exact(inverse, r["spec"][...]), inverse, ((1,), (1,))) / F32(patches)
    for d in sends:
        d.wait_send()


def body(grid, green, sketch):
    C, X, Y, Z = grid
    rows, rank = sketch.shape
    pixels, patches = green.shape
    half_a = (rows // 2 + 7) // 8 * 8
    half_b = rows - half_a
    plane = X * Y - 1

    def vmem(*shape):
        return pltpu.VMEM(shape, F32)

    def dma(*shape):
        return pltpu.SemaphoreType.DMA(shape)

    per_slab = 2 * (X - 1) + 2 * (Y - 1) + 1
    sends = 2 * (Z * per_slab + Z - 1) + 2 * (2 + plane + Z - 1)
    scratch = dict(
        gat=vmem(Z, Y, X, C, rows, rank), sketched=vmem(pixels, rank),
        part=vmem(Z, Y, X, C, rows, rank), rd=vmem(Z, Y, X, rows, rank),
        q=vmem(Z, Y, X, rows, rank),
        rya=vmem(Z, Y, X, half_a, rank), rxb=vmem(Z, X, Y, half_b, rank),
        qa=vmem(Z, X, half_a, rank), qb=vmem(Z, Y, half_b, rank),
        rxa=vmem(Z, X, half_a, rank), ryb=vmem(Z, Y, half_b, rank),
        fin=vmem(Z, rows, rank), rz=vmem(Z, rows, rank),
        ar_src=vmem(2, rank, rank), ar_in=vmem(2, rank // C, rank),
        ar_mid=vmem(2, X * Y, rank // C, rank), ar_top=vmem(2, Z, rank // C, rank),
        gram=vmem(rank, rank), spec=vmem(rank, rank), aug=vmem(rank, 2 * rank),
        send=dma(sends),
        agz=dma(Z), agxa=dma(Z, X), agyb=dma(Z, Y), agya=dma(Z, Y), agxb=dma(Z, X), agd=dma(Z),
        rsd=dma(Z), rsya=dma(Z, Y), rsxb=dma(Z, X), rsxa=dma(Z, X), rsyb=dma(Z, Y), rsz=dma(Z),
        ar0=dma(2), ar1=dma(2, plane), ar2=dma(2, Z), ar3=dma(2),
    )
    total_pixels = pixels * C * X * Y * Z
    return pl.pallas_call(
        functools.partial(kernel, grid, total_pixels, patches),
        out_shape=(
            jax.ShapeDtypeStruct((pixels, rank), F32),
            jax.ShapeDtypeStruct((rows, rank), F32),
            jax.ShapeDtypeStruct((rank, rank), F32),
        ),
        in_specs=[pl.BlockSpec(memory_space=pltpu.VMEM)] * 2,
        out_specs=(pl.BlockSpec(memory_space=pltpu.VMEM),) * 3,
        scratch_shapes=[scratch],
        compiler_params=pltpu.CompilerParams(
            collective_id=0, has_side_effects=True, vmem_limit_bytes=60 * 1024 * 1024
        ),
    )(green, sketch)


def solution(mesh):
    grid = grid_of(mesh.shape["pix"])
    in_specs = (P("pix", None), P("pix", None))
    out_specs = (P("pix", None), P("pix", None), P())
    return jax.shard_map(
        functools.partial(body, grid), mesh=mesh, in_specs=in_specs, out_specs=out_specs, check_vma=False
    )
```

time: 440 us -> 76.3 us (0.17)
  waiting for transfers between devices: 382 us -> 0 us
  Pallas kernels: 0 us -> 70.3 us
  other arithmetic: 25.2 us -> 0 us
  between operations: 13.8 us -> 0.64 us
  matrix products: 12.2 us -> 0 us
    psum x2 -> x0, waiting for transfers between devices: 233 us -> none  [the longest x1 121 us: body(): spectrum_gram = lax.psum(local_spec, 'pix') / jnp.float32(PATCHES)]
    unnamed x5 -> x0, waiting for transfers between devices: 85 us -> none
    pallas_call x0 -> x1, Pallas kernels: none -> 70.3 us  [body(): pl.pallas_call(functools.partial(kernel, grid, total_pixels, patches), ou...]
    all_gather x1 -> x0, waiting for transfers between devices: 64.7 us -> none  [body(): lax.all_gather(sketch, 'pix', axis=0, tiled=True)]
    another operation x5 -> x0, other arithmetic: 22.9 us -> none  [the longest x3 12.4 us: body(): lower = jnp.linalg.cholesky(gram)]
    dot_general x4 -> x0, matrix products: 10.3 us -> none  [the longest x1 4.36 us: body(): lax.dot_general(columns, sketched, (((0,), (0,)), ((), ())), precision=hi...]
  transfers between devices with their start and end apart: 4 -> 0, of which waited for: 4 -> 0; matrix products, arithmetic and copies ran while one was open for 8% -> 0% of each run, Pallas kernels for 0% -> 0%
where the time goes in v1:
time: 76.3 us; the launch traced here: 75.3 us
  Pallas kernels  70.3 us (92%)
  local copies, waits for them, and re-layouts  4.39 us (6%)
    pallas_call x1, Pallas kernels, body(): pl.pallas_call(functools.partial(kernel, grid, total_pixels, patches), ou...  70.3 us
    unnamed x3, local copies, waits for them, and re-layouts  4.39 us

profile of v1, /device:TPU:0, one launch (start us, length us, event | category | flops | bytes accessed | tf_op | source)
XLA Modules:
  0.0 75.3 jit_solution(10148343882163228389)
XLA Ops:
  0.6 70.3 %shard_map.49 = (f32[64,128]{1,0:T(8,128)}, f32[192,128]{1,0:T(8,128)}, f32[128,128]{1,0:T(8,128)}) custom-call(f32[64,6144]{1,0:T(8,128)} %green.1, f32[192,128]{1,0:T(8,128)} %sketch.1), custom_call_target="tpu_custom_call" | custom-call | tf_op jit(solution)/shard_map/pallas_call | solution.py:333
  70.9 1.4 %copy.8 = f32[64,128]{1,0:T(8,128)} copy(f32[64,128]{1,0:T(8,128)} %get-tuple-element.6) | data formatting | bytes 65536
  72.3 1.5 %copy.9 = f32[192,128]{1,0:T(8,128)} copy(f32[192,128]{1,0:T(8,128)} %get-tuple-element.7) | data formatting | bytes 196608
  73.8 1.5 %copy.10 = f32[128,128]{1,0:T(8,128)} copy(f32[128,128]{1,0:T(8,128)} %get-tuple-element.8) | data formatting | bytes 131072

commit v2 on v1

--- a/solution.py
+++ b/solution.py
@@ -10,7 +10,6 @@
 MESH = pl.DeviceIdType.MESH
 F32 = jnp.float32
 BF16 = jnp.bfloat16
-CHUNKS = 4
 
 
 def grid_of(devices):
@@ -38,7 +37,7 @@
     )
 
 
-def kernel(grid, total_pixels, patches, green, sketch, basis, projection, spectrum, scratch):
+def kernel(grid, total_pixels, green_in, sketch_in, basis, projection, inverse_out, spec, scratch):
     C, X, Y, Z = grid
     assert C == 2
     r = scratch
@@ -47,6 +46,11 @@
     x = lax.rem(me // C, X)
     y = lax.rem(me // (C * X), Y)
     z = me // (C * X * Y)
+    green, sketch = r["green"], r["sketch"]
+    load_sketch = pltpu.make_async_copy(sketch_in, sketch, r["load"].at[0])
+    load_green = pltpu.make_async_copy(green_in, green, r["load"].at[1])
+    load_sketch.start()
+    load_green.start()
     rows = sketch.shape[0]
     rank = sketch.shape[1]
     pixels = green.shape[0]
@@ -86,19 +90,26 @@
     peers += [dev(at(z, d, Z), y, x, c) for d in range(1, Z)]
     for peer in peers:
         pl.semaphore_signal(barrier, inc=1, device_id=peer, device_id_type=MESH)
+    load_sketch.wait()
     pl.semaphore_wait(barrier, len(peers))
 
-    near_first = sorted(range(1, Z), key=lambda d: min(d, Z - d))
+    short = jnp.minimum(z, Z - 1 - z)
+    side = jnp.where(z <= Z - 1 - z, 1, -1)
+
+    def near(p):
+        sign = side if p % 2 else -side
+        return z + jnp.where(p <= 2 * short, sign * ((p + 1) // 2), side * (p - short))
+
+    others = range(1, Z)
 
     gat = r["gat"]
-    slabs = [0] + near_first
 
     def ag1(s):
-        zc = at(z, s, Z)
+        zc = near(s)
         if s == 0:
             mine_a, mine_b = sketch.at[part_a], sketch.at[part_b]
         else:
-            arrive(gat.at[zc, y, x, c], r["agz"].at[s])
+            arrive(gat.at[zc, y, x, c], r["agz"].at[zc])
             mine_a, mine_b = gat.at[zc, y, x, c, part_a], gat.at[zc, y, x, c, part_b]
         for dx in range(1, X):
             copy(mine_a, gat.at[zc, y, x, c, part_a], r["agxa"].at[s, dx],
@@ -107,12 +118,12 @@
             copy(mine_b, gat.at[zc, y, x, c, part_b], r["agyb"].at[s, dy],
                  dev(z, at(y, dy, Y), x, c))
         if s == 0:
-            for d in near_first:
-                copy(sketch, gat.at[z, y, x, c], r["agz"].at[d], dev(at(z, -d, Z), y, x, c))
+            for p in others:
+                copy(sketch, gat.at[z, y, x, c], r["agz"].at[z], dev(near(p), y, x, c))
             gat[z, y, x, c] = sketch[...]
 
     def ag2(s):
-        zc = at(z, s, Z)
+        zc = near(s)
         for dx in range(1, X):
             arrive(gat.at[zc, y, at(x, -dx, X), c, part_a], r["agxa"].at[s, dx])
         for dy in range(1, Y):
@@ -125,7 +136,7 @@
             copy(ref, ref, r["agxb"].at[s, dx], dev(z, y, at(x, dx, X), c))
 
     def ag3(s):
-        zc = at(z, s, Z)
+        zc = near(s)
         for dy in range(1, Y):
             arrive(gat.at[zc, at(y, -dy, Y), :, c, part_a], r["agya"].at[s, dy])
         for dx in range(1, X):
@@ -134,8 +145,10 @@
         copy(ref, ref, r["agd"].at[s], partner)
 
     def ag4(s):
-        zc = at(z, s, Z)
+        zc = near(s)
         arrive(gat.at[zc, :, :, 1 - c], r["agd"].at[s])
+        if s == 0:
+            load_green.wait()
         block = gat[zc].reshape(slab, rank)
         g = green[:, pl.ds(pl.multiple_of(zc * slab, 128), slab)]
         g_hi, g_lo = split(g)
@@ -147,17 +160,15 @@
         else:
             r["sketched"][...] += out
 
-    def pipeline(stages, items, extra=()):
-        extra = list(extra)
+    def pipeline(stages, items, extra):
         for t in range(len(items) + len(stages) - 1):
             for k, stage in enumerate(stages):
                 if 0 <= t - k < len(items):
                     stage(items[t - k])
-            if t > 0 and extra:
-                extra.pop(0)()
-        return extra
-
-    pipeline([ag1, ag2, ag3, ag4], slabs)
+            for job in extra.get(t, ()):
+                job()
+
+    pipeline([ag1, ag2, ag3, ag4], range(Z), {})
     sketched = r["sketched"][...]
     s_hi, s_lo = split(sketched)
     packed = jnp.concatenate([s_hi, s_lo, s_hi, s_lo], axis=0)
@@ -184,12 +195,12 @@
             for i, (dy, dx) in enumerate(plane):
                 arrive(mid.at[at(y, -dy, Y) * X + at(x, -dx, X)], r["ar1"].at[k, i])
             top[z] = jnp.sum(mid[...], axis=0)
-            for d in near_first:
-                copy(top.at[z], top.at[z], r["ar2"].at[k, d], dev(at(z, d, Z), y, x, c))
+            for p in others:
+                copy(top.at[z], top.at[z], r["ar2"].at[k, z], dev(near(p), y, x, c))
 
         def step3():
-            for d in near_first:
-                arrive(top.at[at(z, -d, Z)], r["ar2"].at[k, d])
+            for p in others:
+                arrive(top.at[near(p)], r["ar2"].at[k, near(p)])
             out[keep, :] = jnp.sum(top[...], axis=0)
             copy(out.at[keep], out.at[keep], r["ar3"].at[k], partner)
 
@@ -211,19 +222,27 @@
         aug[...] = aug[...] - f * row
         return 0
 
-    def chol(i):
+    def begin():
+        aug[:, :rank] = r["gram"][...]
+        aug[:, rank:] = jnp.where(lane == row_of, 1.0, 0.0)
+
+    def chol(first, last):
         def run():
-            if i == 0:
-                aug[:, :rank] = r["gram"][...]
-                aug[:, rank:] = jnp.where(lane == row_of, 1.0, 0.0)
-            lax.fori_loop(rank // CHUNKS * i, rank // CHUNKS * (i + 1), eliminate, 0)
+            lax.fori_loop(first, last, eliminate, 0)
 
         return run
 
+    def finish():
+        diag = jnp.sum(jnp.where(lane == row_of, aug[:, :rank], 0.0), axis=1, keepdims=True)
+        inverse = aug[:, rank:] * lax.rsqrt(diag)
+        inverse_out[...] = inverse
+        basis[...] = jnp.sqrt(F32(total_pixels)) * exact(sketched, inverse, ((1,), (1,)))
+        projection[...] = exact(raw, inverse, ((1,), (1,)))
+
     part, q = r["part"], r["q"]
 
     def rs1(s):
-        zo = at(z, s, Z)
+        zo = near(s)
         g_hi, g_lo = split(green[:, pl.ds(pl.multiple_of(zo * slab, 128), slab)])
         tall = jnp.concatenate([g_hi, g_hi, g_lo, g_lo], axis=0)
         part[s] = dot(tall, packed, ((0,), (0,))).reshape(Y, X, C, rows, rank)
@@ -269,32 +288,41 @@
             total = total + r["ryb"][s, dy]
         r["fin"][s, part_b] = total
         if s:
-            copy(r["fin"].at[s], r["rz"].at[s], r["rsz"].at[s], dev(at(z, s, Z), y, x, c))
+            copy(r["fin"].at[s], r["rz"].at[z], r["rsz"].at[z], dev(near(s), y, x, c))
+
+    def cut(k):
+        return rank * k // 16
 
     gram_sum = all_sum(0, lambda: exact(sketched, sketched, ((0,), (0,))), r["gram"])
     gram_sum[0]()
-    todo = gram_sum[1:] + [chol(i) for i in range(CHUNKS)]
-    todo = pipeline([rs1, rs2, rs3, rs4], near_first[::-1] + [0], todo)
+    last = Z + 2
+    extra = {1: gram_sum[1:2], last - 3: gram_sum[2:3], last - 1: gram_sum[3:4],
+             last: gram_sum[4:5] + [begin, chol(0, cut(2))]}
+    pipeline([rs1, rs2, rs3, rs4], range(Z)[::-1], extra)
 
     raw = r["fin"][0]
-    for s in range(1, Z):
-        arrive(r["rz"].at[s], r["rsz"].at[s])
-        raw = raw + r["rz"][s]
-    spec_sum = all_sum(1, lambda: exact(raw, raw, ((0,), (0,))), r["spec"])
-    for k, step in enumerate(spec_sum):
-        step()
-        if todo:
-            todo.pop(0)()
-    for job in todo:
-        job()
-
-    diag = jnp.sum(jnp.where(lane == row_of, aug[:, :rank], 0.0), axis=1, keepdims=True)
-    inverse = aug[:, rank:] * lax.rsqrt(diag)
-    basis[...] = jnp.sqrt(F32(total_pixels)) * exact(sketched, inverse, ((1,), (1,)))
-    projection[...] = exact(raw, inverse, ((1,), (1,)))
-    spectrum[...] = exact(exact(inverse, r["spec"][...]), inverse, ((1,), (1,))) / F32(patches)
+    for p in others:
+        arrive(r["rz"].at[near(p)], r["rsz"].at[near(p)])
+        raw = raw + r["rz"][near(p)]
+    spec_sum = all_sum(1, lambda: exact(raw, raw, ((0,), (0,))), spec)
+    spec_sum[0]()
+    chol(cut(2), cut(4))()
+    spec_sum[1]()
+    chol(cut(4), cut(9))()
+    spec_sum[2]()
+    chol(cut(9), cut(16))()
+    spec_sum[3]()
+    finish()
+    spec_sum[4]()
     for d in sends:
         d.wait_send()
+
+
+def finish_kernel(patches, basis_in, projection_in, inverse_in, spec_in, basis, projection, spectrum):
+    inverse = inverse_in[...]
+    basis[...] = basis_in[...]
+    projection[...] = projection_in[...]
+    spectrum[...] = exact(exact(inverse, spec_in[...]), inverse, ((1,), (1,))) / F32(patches)
 
 
 def body(grid, green, sketch):
@@ -323,27 +351,33 @@
         fin=vmem(Z, rows, rank), rz=vmem(Z, rows, rank),
         ar_src=vmem(2, rank, rank), ar_in=vmem(2, rank // C, rank),
         ar_mid=vmem(2, X * Y, rank // C, rank), ar_top=vmem(2, Z, rank // C, rank),
-        gram=vmem(rank, rank), spec=vmem(rank, rank), aug=vmem(rank, 2 * rank),
-        send=dma(sends),
+        gram=vmem(rank, rank), green=vmem(pixels, patches), sketch=vmem(rows, rank), aug=vmem(rank, 2 * rank),
+        send=dma(sends), load=dma(2),
         agz=dma(Z), agxa=dma(Z, X), agyb=dma(Z, Y), agya=dma(Z, Y), agxb=dma(Z, X), agd=dma(Z),
         rsd=dma(Z), rsya=dma(Z, Y), rsxb=dma(Z, X), rsxa=dma(Z, X), rsyb=dma(Z, Y), rsz=dma(Z),
         ar0=dma(2), ar1=dma(2, plane), ar2=dma(2, Z), ar3=dma(2),
     )
     total_pixels = pixels * C * X * Y * Z
-    return pl.pallas_call(
-        functools.partial(kernel, grid, total_pixels, patches),
-        out_shape=(
-            jax.ShapeDtypeStruct((pixels, rank), F32),
-            jax.ShapeDtypeStruct((rows, rank), F32),
-            jax.ShapeDtypeStruct((rank, rank), F32),
-        ),
-        in_specs=[pl.BlockSpec(memory_space=pltpu.VMEM)] * 2,
-        out_specs=(pl.BlockSpec(memory_space=pltpu.VMEM),) * 3,
+    tall = jax.ShapeDtypeStruct((pixels, rank), F32)
+    wide = jax.ShapeDtypeStruct((rows, rank), F32)
+    square = jax.ShapeDtypeStruct((rank, rank), F32)
+    whole = pl.BlockSpec(memory_space=pltpu.VMEM)
+    parts = pl.pallas_call(
+        functools.partial(kernel, grid, total_pixels),
+        out_shape=(tall, wide, square, square),
+        in_specs=[pl.BlockSpec(memory_space=pl.ANY)] * 2,
+        out_specs=(whole,) * 4,
         scratch_shapes=[scratch],
         compiler_params=pltpu.CompilerParams(
-            collective_id=0, has_side_effects=True, vmem_limit_bytes=60 * 1024 * 1024
+            collective_id=0, has_side_effects=True, vmem_limit_bytes=63 * 1024 * 1024
         ),
     )(green, sketch)
+    return pl.pallas_call(
+        functools.partial(finish_kernel, patches),
+        out_shape=(tall, wide, square),
+        in_specs=[whole] * 4,
+        out_specs=(whole,) * 3,
+    )(*parts)
 
 
 def solution(mesh):

time: 76.3 us -> 69.6 us (0.912); the launches traced: 75.3 us -> 69.5 us
  local copies, waits for them, and re-layouts: 4.39 us -> 0 us
  Pallas kernels: 70.3 us -> 68.8 us
    unnamed x3 -> x0, local copies, waits for them, and re-layouts: 4.39 us -> none
    pallas_call x1 -> x2, Pallas kernels: 70.3 us -> 68.8 us  [the longest x1 66.8 us: body(): pl.pallas_call(functools.partial(kernel, grid, total_pixels), out_shape=(...]
where the time goes in v2:
time: 69.6 us; the launch traced here: 69.5 us
  Pallas kernels  68.8 us (99%)
    pallas_call x1, Pallas kernels, body(): pl.pallas_call(functools.partial(kernel, grid, total_pixels), out_shape=(...  66.8 us
    pallas_call x1, Pallas kernels, body(): pl.pallas_call(functools.partial(finish_kernel, patches), out_shape=(tall...  2.07 us

profile of v2, /device:TPU:0, one launch (start us, length us, event | category | flops | bytes accessed | tf_op | source)
XLA Modules:
  0.0 69.5 jit_solution(11947059537639289795)
XLA Ops:
  0.6 66.8 %shard_map.49 = (f32[64,128]{1,0:T(8,128)}, f32[192,128]{1,0:T(8,128)}, f32[128,128]{1,0:T(8,128)}, f32[128,128]{1,0:T(8,128)}) custom-call(f32[64,6144]{1,0:T(8,128)} %green_in.1, f32[192,128]{1,0:T(8,128)} %sketch_in.1), custom_call_target="tpu_custom_call" | custom-call | tf_op jit(solution)/shard_map/pallas_call | solution.py:365
  67.4 2.1 %shard_map.50 = (f32[64,128]{1,0:T(8,128)}, f32[192,128]{1,0:T(8,128)}, f32[128,128]{1,0:T(8,128)}) custom-call(f32[64,128]{1,0:T(8,128)} %get-tuple-element.7.basis_in, f32[192,128]{1,0:T(8,128)} %get-tuple-element.8.projection_in, f32[128,128]{1,0:T(8,128)} %get-tuple-element.9.inverse_in, f32[128,128]{1,0:T(8,128)} %get-tuple-element.10.spec_in), custom_call_target="tpu_custom_call" | custom-call | tf_op jit(solution)/shard_map/pallas_call | solution.py:375

commit v3 on v2

--- a/solution.py
+++ b/solution.py
@@ -10,6 +10,7 @@
 MESH = pl.DeviceIdType.MESH
 F32 = jnp.float32
 BF16 = jnp.bfloat16
+PANEL = 8
 
 
 def grid_of(devices):
@@ -25,6 +26,12 @@
 def split(v):
     hi = v.astype(BF16)
     return hi, (v - hi.astype(F32)).astype(BF16)
+
+
+def thirds(v):
+    a = v.astype(BF16).astype(F32)
+    b = (v - a).astype(BF16).astype(F32)
+    return a, b, v - a - b
 
 
 def dot(a, b, dims=((1,), (0,))):
@@ -173,64 +180,91 @@
     s_hi, s_lo = split(sketched)
     packed = jnp.concatenate([s_hi, s_lo, s_hi, s_lo], axis=0)
 
-    def all_sum(k, value, out):
-        inc, mid, top = r["ar_in"].at[k], r["ar_mid"].at[k], r["ar_top"].at[k]
-        h = rank // C
-        keep = pl.ds(pl.multiple_of(c * h, h), h)
-        give = pl.ds(pl.multiple_of((1 - c) * h, h), h)
+    def spread_sum(k, value):
         here = y * X + x
+        q = rank // (C * X * Y)
+        src, inc, red, mid, top, res = (r[n].at[k] for n in ("s_src", "s_in", "s_red", "s_mid", "s_top", "s_res"))
 
         def step0():
-            r["ar_src"][k] = value()
-            copy(r["ar_src"].at[k, give], inc, r["ar0"].at[k], partner)
+            v = value()
+            for i in range(C):
+                for w in range(X * Y):
+                    first = (i * X * Y + w) * q
+                    src[i, w] = v[first : first + q]
+            copy(src.at[1 - c], inc, r["sp0"].at[k], partner)
 
         def step1():
-            arrive(inc, r["ar0"].at[k])
-            mid[here] = r["ar_src"][k, keep] + inc[...]
+            arrive(inc, r["sp0"].at[k])
+            red[...] = src[c] + inc[...]
+            mid[here] = red[here]
             for i, (dy, dx) in enumerate(plane):
-                copy(mid.at[here], mid.at[here], r["ar1"].at[k, i],
-                     dev(z, at(y, dy, Y), at(x, dx, X), c))
+                yy, xx = at(y, dy, Y), at(x, dx, X)
+                copy(red.at[yy * X + xx], mid.at[here], r["sp1"].at[k, i], dev(z, yy, xx, c))
 
         def step2():
             for i, (dy, dx) in enumerate(plane):
-                arrive(mid.at[at(y, -dy, Y) * X + at(x, -dx, X)], r["ar1"].at[k, i])
+                arrive(mid.at[at(y, -dy, Y) * X + at(x, -dx, X)], r["sp1"].at[k, i])
             top[z] = jnp.sum(mid[...], axis=0)
             for p in others:
-                copy(top.at[z], top.at[z], r["ar2"].at[k, z], dev(near(p), y, x, c))
+                copy(top.at[z], top.at[z], r["sp2"].at[k, z], dev(near(p), y, x, c))
 
         def step3():
             for p in others:
-                arrive(top.at[near(p)], r["ar2"].at[k, near(p)])
-            out[keep, :] = jnp.sum(top[...], axis=0)
-            copy(out.at[keep], out.at[keep], r["ar3"].at[k], partner)
+                arrive(top.at[near(p)], r["sp2"].at[k, near(p)])
+            res[c, here] = jnp.sum(top[...], axis=0)
+            for i, (dy, dx) in enumerate(plane):
+                copy(res.at[c, here], res.at[c, here], r["sp3"].at[k, i],
+                     dev(z, at(y, dy, Y), at(x, dx, X), c))
 
         def step4():
-            arrive(out.at[give], r["ar3"].at[k])
-
-        return [step0, step1, step2, step3, step4]
+            for i, (dy, dx) in enumerate(plane):
+                arrive(res.at[c, at(y, -dy, Y) * X + at(x, -dx, X)], r["sp3"].at[k, i])
+            copy(res.at[c], res.at[c], r["sp4"].at[k], partner)
+
+        def step5():
+            arrive(res.at[1 - c], r["sp4"].at[k])
+
+        def total():
+            return jnp.concatenate([res[i, w] for i in range(C) for w in range(X * Y)], axis=0)
+
+        return [step0, step1, step2, step3, step4, step5], total
 
     aug = r["aug"]
     lane = lax.broadcasted_iota(jnp.int32, (rank, rank), 1)
     row_of = lax.broadcasted_iota(jnp.int32, (rank, rank), 0)
 
-    def eliminate(j, _):
-        row = aug[pl.ds(j, 1), :]
-        left = aug[:, :rank]
-        col = jnp.sum(jnp.where(lane == j, left, 0.0), axis=1, keepdims=True)
-        pivot = jnp.sum(jnp.where(lane[:1] == j, row[:, :rank], 0.0), axis=1, keepdims=True)
-        f = jnp.where(row_of[:, :1] > j, col * (1.0 / pivot), 0.0)
-        aug[...] = aug[...] - f * row
+    def eliminate(p, _):
+        first = pl.multiple_of(p * PANEL, PANEL)
+        lanes = lane[:PANEL]
+        index = row_of[:PANEL, :1]
+        block = aug[pl.ds(first, PANEL), :]
+        left = block[:, :rank]
+        cols = [
+            jnp.sum(jnp.where(lanes == first + k, left, 0.0), axis=1, keepdims=True)
+            for k in range(PANEL)
+        ]
+        scale = jnp.zeros((PANEL, 1), F32)
+        for k in range(PANEL):
+            inv = 1.0 / cols[k][k : k + 1]
+            f = jnp.where(index > k, cols[k] * inv, 0.0)
+            for m in range(k + 1, PANEL):
+                cols[m] = cols[m] - f * cols[m][k : k + 1]
+            block = block - f * block[k : k + 1]
+            scale = jnp.where(index == k, inv, scale)
+        u = thirds(jnp.where(lanes >= first + PANEL, block[:, :rank] * scale, 0.0))
+        v = thirds(block)
+        lhs = jnp.concatenate([u[i] for i in (0, 0, 0, 1, 1, 2)], axis=0).astype(BF16)
+        rhs = jnp.concatenate([v[i] for i in (0, 1, 2, 0, 1, 0)], axis=0).astype(BF16)
+        aug[...] = aug[...] - dot(lhs, rhs, ((0,), (0,)))
+        aug[pl.ds(first, PANEL), :] = block
         return 0
 
     def begin():
-        aug[:, :rank] = r["gram"][...]
+        aug[:, :rank] = gram_total()
         aug[:, rank:] = jnp.where(lane == row_of, 1.0, 0.0)
 
     def chol(first, last):
-        def run():
-            lax.fori_loop(first, last, eliminate, 0)
-
-        return run
+        lax.fori_loop(first, last, eliminate, 0)
 
     def finish():
         diag = jnp.sum(jnp.where(lane == row_of, aug[:, :rank], 0.0), axis=1, keepdims=True)
@@ -290,30 +324,30 @@
         if s:
             copy(r["fin"].at[s], r["rz"].at[z], r["rsz"].at[z], dev(near(s), y, x, c))
 
-    def cut(k):
-        return rank * k // 16
-
-    gram_sum = all_sum(0, lambda: exact(sketched, sketched, ((0,), (0,))), r["gram"])
-    gram_sum[0]()
+    gram, gram_total = spread_sum(0, lambda: exact(sketched, sketched, ((0,), (0,))))
     last = Z + 2
-    extra = {1: gram_sum[1:2], last - 3: gram_sum[2:3], last - 1: gram_sum[3:4],
-             last: gram_sum[4:5] + [begin, chol(0, cut(2))]}
+    extra = {0: gram[:1], 1: gram[1:2], last - 3: gram[2:3], last - 1: gram[3:4], last: gram[4:5]}
     pipeline([rs1, rs2, rs3, rs4], range(Z)[::-1], extra)
 
     raw = r["fin"][0]
     for p in others:
         arrive(r["rz"].at[near(p)], r["rsz"].at[near(p)])
         raw = raw + r["rz"][near(p)]
-    spec_sum = all_sum(1, lambda: exact(raw, raw, ((0,), (0,))), spec)
+    spec_sum, spec_total = spread_sum(1, lambda: exact(raw, raw, ((0,), (0,))))
+    panels = rank // PANEL
     spec_sum[0]()
-    chol(cut(2), cut(4))()
+    gram[5]()
+    begin()
     spec_sum[1]()
-    chol(cut(4), cut(9))()
+    chol(0, panels * 2 // 5)
     spec_sum[2]()
-    chol(cut(9), cut(16))()
+    chol(panels * 2 // 5, panels * 4 // 5)
     spec_sum[3]()
+    chol(panels * 4 // 5, panels)
     finish()
     spec_sum[4]()
+    spec_sum[5]()
+    spec[...] = spec_total()
     for d in sends:
         d.wait_send()
 
@@ -332,6 +366,7 @@
     half_a = (rows // 2 + 7) // 8 * 8
     half_b = rows - half_a
     plane = X * Y - 1
+    few = rank // (C * X * Y)
 
     def vmem(*shape):
         return pltpu.VMEM(shape, F32)
@@ -340,7 +375,7 @@
         return pltpu.SemaphoreType.DMA(shape)
 
     per_slab = 2 * (X - 1) + 2 * (Y - 1) + 1
-    sends = 2 * (Z * per_slab + Z - 1) + 2 * (2 + plane + Z - 1)
+    sends = 2 * (Z * per_slab + Z - 1) + 2 * (2 + 2 * plane + Z - 1)
     scratch = dict(
         gat=vmem(Z, Y, X, C, rows, rank), sketched=vmem(pixels, rank),
         part=vmem(Z, Y, X, C, rows, rank), rd=vmem(Z, Y, X, rows, rank),
@@ -349,13 +384,14 @@
         qa=vmem(Z, X, half_a, rank), qb=vmem(Z, Y, half_b, rank),
         rxa=vmem(Z, X, half_a, rank), ryb=vmem(Z, Y, half_b, rank),
         fin=vmem(Z, rows, rank), rz=vmem(Z, rows, rank),
-        ar_src=vmem(2, rank, rank), ar_in=vmem(2, rank // C, rank),
-        ar_mid=vmem(2, X * Y, rank // C, rank), ar_top=vmem(2, Z, rank // C, rank),
-        gram=vmem(rank, rank), green=vmem(pixels, patches), sketch=vmem(rows, rank), aug=vmem(rank, 2 * rank),
+        s_src=vmem(2, C, X * Y, few, rank), s_in=vmem(2, X * Y, few, rank),
+        s_red=vmem(2, X * Y, few, rank), s_mid=vmem(2, X * Y, few, rank),
+        s_top=vmem(2, Z, few, rank), s_res=vmem(2, C, X * Y, few, rank),
+        green=vmem(pixels, patches), sketch=vmem(rows, rank), aug=vmem(rank, 2 * rank),
         send=dma(sends), load=dma(2),
         agz=dma(Z), agxa=dma(Z, X), agyb=dma(Z, Y), agya=dma(Z, Y), agxb=dma(Z, X), agd=dma(Z),
         rsd=dma(Z), rsya=dma(Z, Y), rsxb=dma(Z, X), rsxa=dma(Z, X), rsyb=dma(Z, Y), rsz=dma(Z),
-        ar0=dma(2), ar1=dma(2, plane), ar2=dma(2, Z), ar3=dma(2),
+        sp0=dma(2), sp1=dma(2, plane), sp2=dma(2, Z), sp3=dma(2, plane), sp4=dma(2),
     )
     total_pixels = pixels * C * X * Y * Z
     tall = jax.ShapeDtypeStruct((pixels, rank), F32)

time: 69.6 us -> 63.8 us (0.917)
  Pallas kernels: 68.8 us -> 63 us
    pallas_call x1, Pallas kernels: 66.8 us -> 60.9 us  [body(): pl.pallas_call(functools.partial(kernel, grid, total_pixels), out_shape=(...]
where the time goes in v3:
time: 63.8 us; the launch traced here: 63.6 us
  Pallas kernels  63 us (99%)
  between operations  0.64 us (1%)
    pallas_call x1, Pallas kernels, body(): pl.pallas_call(functools.partial(kernel, grid, total_pixels), out_shape=(...  60.9 us
    pallas_call x1, Pallas kernels, body(): pl.pallas_call(functools.partial(finish_kernel, patches), out_shape=(tall...  2.07 us

profile of v3, /device:TPU:0, one launch (start us, length us, event | category | flops | bytes accessed | tf_op | source)
XLA Modules:
  0.0 63.6 jit_solution(15116650190632829621)
XLA Ops:
  0.6 60.9 %shard_map.49 = (f32[64,128]{1,0:T(8,128)}, f32[192,128]{1,0:T(8,128)}, f32[128,128]{1,0:T(8,128)}, f32[128,128]{1,0:T(8,128)}) custom-call(f32[64,6144]{1,0:T(8,128)} %green_in.1, f32[192,128]{1,0:T(8,128)} %sketch_in.1), custom_call_target="tpu_custom_call" | custom-call | tf_op jit(solution)/shard_map/pallas_call | solution.py:401
  61.5 2.1 %shard_map.50 = (f32[64,128]{1,0:T(8,128)}, f32[192,128]{1,0:T(8,128)}, f32[128,128]{1,0:T(8,128)}) custom-call(f32[64,128]{1,0:T(8,128)} %get-tuple-element.7.basis_in, f32[192,128]{1,0:T(8,128)} %get-tuple-element.8.projection_in, f32[128,128]{1,0:T(8,128)} %get-tuple-element.9.inverse_in, f32[128,128]{1,0:T(8,128)} %get-tuple-element.10.spec_in), custom_call_target="tpu_custom_call" | custom-call | tf_op jit(solution)/shard_map/pallas_call | solution.py:411

commit v4 on v3

--- a/solution.py
+++ b/solution.py
@@ -179,6 +179,42 @@
     sketched = r["sketched"][...]
     s_hi, s_lo = split(sketched)
     packed = jnp.concatenate([s_hi, s_lo, s_hi, s_lo], axis=0)
+
+    def all_sum(k, value, out):
+        inc, mid, top = r["ar_in"].at[k], r["ar_mid"].at[k], r["ar_top"].at[k]
+        h = rank // C
+        keep = pl.ds(pl.multiple_of(c * h, h), h)
+        give = pl.ds(pl.multiple_of((1 - c) * h, h), h)
+        here = y * X + x
+
+        def step0():
+            r["ar_src"][k] = value()
+            copy(r["ar_src"].at[k, give], inc, r["ar0"].at[k], partner)
+
+        def step1():
+            arrive(inc, r["ar0"].at[k])
+            mid[here] = r["ar_src"][k, keep] + inc[...]
+            for i, (dy, dx) in enumerate(plane):
+                copy(mid.at[here], mid.at[here], r["ar1"].at[k, i],
+                     dev(z, at(y, dy, Y), at(x, dx, X), c))
+
+        def step2():
+            for i, (dy, dx) in enumerate(plane):
+                arrive(mid.at[at(y, -dy, Y) * X + at(x, -dx, X)], r["ar1"].at[k, i])
+            top[z] = jnp.sum(mid[...], axis=0)
+            for p in others:
+                copy(top.at[z], top.at[z], r["ar2"].at[k, z], dev(near(p), y, x, c))
+
+        def step3():
+            for p in others:
+                arrive(top.at[near(p)], r["ar2"].at[k, near(p)])
+            out[keep, :] = jnp.sum(top[...], axis=0)
+            copy(out.at[keep], out.at[keep], r["ar3"].at[k], partner)
+
+        def step4():
+            arrive(out.at[give], r["ar3"].at[k])
+
+        return [step0, step1, step2, step3, step4]
 
     def spread_sum(k, value):
         here = y * X + x
@@ -333,7 +369,7 @@
     for p in others:
         arrive(r["rz"].at[near(p)], r["rsz"].at[near(p)])
         raw = raw + r["rz"][near(p)]
-    spec_sum, spec_total = spread_sum(1, lambda: exact(raw, raw, ((0,), (0,))))
+    spec_sum = all_sum(0, lambda: exact(raw, raw, ((0,), (0,))), spec)
     panels = rank // PANEL
     spec_sum[0]()
     gram[5]()
@@ -341,13 +377,10 @@
     spec_sum[1]()
     chol(0, panels * 2 // 5)
     spec_sum[2]()
-    chol(panels * 2 // 5, panels * 4 // 5)
+    chol(panels * 2 // 5, panels)
     spec_sum[3]()
-    chol(panels * 4 // 5, panels)
     finish()
     spec_sum[4]()
-    spec_sum[5]()
-    spec[...] = spec_total()
     for d in sends:
         d.wait_send()
 
@@ -384,6 +417,8 @@
         qa=vmem(Z, X, half_a, rank), qb=vmem(Z, Y, half_b, rank),
         rxa=vmem(Z, X, half_a, rank), ryb=vmem(Z, Y, half_b, rank),
         fin=vmem(Z, rows, rank), rz=vmem(Z, rows, rank),
+        ar_src=vmem(1, rank, rank), ar_in=vmem(1, rank // C, rank),
+        ar_mid=vmem(1, X * Y, rank // C, rank), ar_top=vmem(1, Z, rank // C, rank),
         s_src=vmem(2, C, X * Y, few, rank), s_in=vmem(2, X * Y, few, rank),
         s_red=vmem(2, X * Y, few, rank), s_mid=vmem(2, X * Y, few, rank),
         s_top=vmem(2, Z, few, rank), s_res=vmem(2, C, X * Y, few, rank),
@@ -391,6 +426,7 @@
         send=dma(sends), load=dma(2),
         agz=dma(Z), agxa=dma(Z, X), agyb=dma(Z, Y), agya=dma(Z, Y), agxb=dma(Z, X), agd=dma(Z),
         rsd=dma(Z), rsya=dma(Z, Y), rsxb=dma(Z, X), rsxa=dma(Z, X), rsyb=dma(Z, Y), rsz=dma(Z),
+        ar0=dma(1), ar1=dma(1, plane), ar2=dma(1, Z), ar3=dma(1),
         sp0=dma(2), sp1=dma(2, plane), sp2=dma(2, Z), sp3=dma(2, plane), sp4=dma(2),
     )
     total_pixels = pixels * C * X * Y * Z

time: 63.8 us -> 63.5 us (level)
  no operation moved by 1% of the time
where the time goes in v4:
time: 63.5 us; the launch traced here: 63.3 us
  Pallas kernels  62.7 us (99%)
  between operations  0.64 us (1%)
    pallas_call x1, Pallas kernels, body(): pl.pallas_call(functools.partial(kernel, grid, total_pixels), out_shape=(...  60.6 us
    pallas_call x1, Pallas kernels, body(): pl.pallas_call(functools.partial(finish_kernel, patches), out_shape=(tall...  2.07 us

profile of v4, /device:TPU:0, one launch (start us, length us, event | category | flops | bytes accessed | tf_op | source)
XLA Modules:
  0.0 63.3 jit_solution(9390257459188231001)
XLA Ops:
  0.6 60.6 %shard_map.49 = (f32[64,128]{1,0:T(8,128)}, f32[192,128]{1,0:T(8,128)}, f32[128,128]{1,0:T(8,128)}, f32[128,128]{1,0:T(8,128)}) custom-call(f32[64,6144]{1,0:T(8,128)} %green_in.1, f32[192,128]{1,0:T(8,128)} %sketch_in.1), custom_call_target="tpu_custom_call" | custom-call | tf_op jit(solution)/shard_map/pallas_call | solution.py:437
  61.2 2.1 %shard_map.50 = (f32[64,128]{1,0:T(8,128)}, f32[192,128]{1,0:T(8,128)}, f32[128,128]{1,0:T(8,128)}) custom-call(f32[64,128]{1,0:T(8,128)} %get-tuple-element.7.basis_in, f32[192,128]{1,0:T(8,128)} %get-tuple-element.8.projection_in, f32[128,128]{1,0:T(8,128)} %get-tuple-element.9.inverse_in, f32[128,128]{1,0:T(8,128)} %get-tuple-element.10.spec_in), custom_call_target="tpu_custom_call" | custom-call | tf_op jit(solution)/shard_map/pallas_call | solution.py:447
